TPU v7x, 32 devices: a whole 2x2x4 slice. The times are simulated.
32 devices in a mesh: grp: 4 (over y, x), sub: 8 (over z, core).
Axes of the slice: x: 2, y: 2, z: 4, core: 2. Of those that a mesh axis runs over, the one named last changes fastest.
Arguments:
- initial_field: float32 [4, 16, 16384], P('grp', 'sub'), may hold values from -6 to 6
- conduct: float32 [4, 16, 16384], P('grp', 'sub'), may hold values from 0.02 to 0.12
- velocity: float32 [4, 16, 16384], P('grp', 'sub'), may hold values from 0 to 0.25
- heat_release: float32 [4, 16, 16384], P('grp', 'sub'), may hold values from 0.01 to 0.1
- group_kind: int32 [4], replicated, may hold values from 0 to 1, as said below
- partner: int32 [4], replicated, may hold values from 0 to 3, as said below
- surface_cell: int32 [4, 4096], P('grp', 'sub'), may hold values from 0 to 32767
- patch_count: int32 [4, 8], P('grp'), may hold values from 1 to 24, 64 in all within a row
- patch_centres: int32 [4, 192, 128], P('grp', 'sub'), may hold values from 0 to 4095, as said below
- patch_targets: int32 [4, 192, 128], P('grp', 'sub'), may hold values from 0 to 4095
- patch_maps: float32 [4, 192, 128, 128], P('grp', 'sub'), may hold values from -0.25 to 0.95
Outputs:
- temperature: float32 [4, 16, 16384], P('grp', 'sub')
- interface: float32 [4, 2, 4096], P('grp', None, 'sub')
Inputs may be any that keep to these rules, and one draw needn't show every extreme that they name: `group_kind`: both kinds occur. partner[g] is a group of the other kind than g. Slots 0 to patch_count[g, j] - 1 of device j of group g are live; each group's counts sum to 64; in each group some device holds 24. `patch_centres`: the centres of slot s of group g lie in the cyclic window of 1024 consecutive nodes that starts at (s // 24) * 512 - 512 // 2 + h[g], for one shift h[g] of each group.
All inputs are finite; a program needn't handle non-finite values.
Results may differ from a plain program's by a relative error of at most 0.00013.
Values sent between devices are 32-bit elements; how exact they have to be, the bound alone decides.
A program may use at most 64 MiB of HBM per device.

v0:
```python
import jax
import jax.numpy as jnp
from jax import lax
from jax.sharding import PartitionSpec as P

STEPS = 4
COUPLE = 4


def with_halo(cells, sides, width):
    for axis, dim in sides:
        count = lax.axis_size(axis)
        ends = count - 1
        head = lax.slice_in_dim(cells, 0, width, axis=dim)
        tail = lax.slice_in_dim(cells, cells.shape[dim] - width, cells.shape[dim], axis=dim)
        cells = jnp.concatenate(
            [
                lax.ppermute(tail, axis, [(i, (i + 1) % count) for i in range(ends)]),
                cells,
                lax.ppermute(head, axis, [((i + 1) % count, i) for i in range(ends)]),
            ],
            axis=dim,
        )
    return cells


def in_plane(current):
    return (
        jnp.roll(current, 1, -2)
        + jnp.roll(current, -1, -2)
        + jnp.roll(current, 1, -1)
        + jnp.roll(current, -1, -1)
    )


def advance(padded, conduct, velocity, heat_release, gas_mask):
    centre = padded[1:-1]
    upper_plane = padded[2:]
    lower_plane = padded[:-2]
    laplace = upper_plane + lower_plane + in_plane(centre) - 6.0 * centre
    return (
        centre
        + conduct * laplace
        - gas_mask * velocity * (centre - lower_plane)
        + gas_mask * heat_release * jax.nn.sigmoid(2.0 * centre)
    )


def local(
    initial_field,
    conduct,
    velocity,
    heat_release,
    group_kind,
    partner,
    surface_cell,
    patch_count,
    patch_centres,
    patch_targets,
    patch_maps,
):
    planes_here = initial_field.shape[1]
    plane_cells = initial_field.shape[2]
    slab_shape = (planes_here, plane_cells // 128, 128)
    current = initial_field.reshape(slab_shape)
    conduct_slab = conduct.reshape(slab_shape)
    velocity_slab = velocity.reshape(slab_shape)
    heat_slab = heat_release.reshape(slab_shape)
    sub_count = lax.axis_size("sub")
    slab_index = lax.axis_index("sub")
    group_index = lax.axis_index("grp")
    own_kind = group_kind[group_index]
    partner_row = partner[group_index]
    gas_mask = (own_kind == 0).astype(jnp.float32)
    gain_temp = jnp.where(own_kind == 0, 0.5, 0.25).astype(jnp.float32)
    gain_flux = jnp.where(own_kind == 0, -0.25, 0.25).astype(jnp.float32)
    surface = surface_cell[0]
    counts = patch_count[0]
    patch_mats = patch_maps[0]
    centres = patch_centres[0]
    targets = patch_targets[0]
    surf_here = surface.shape[0]
    node_total = surf_here * sub_count
    capacity = patch_mats.shape[0]
    live_mask = (jnp.arange(capacity, dtype=jnp.int32) < counts[slab_index]).astype(jnp.float32)
    interface = jnp.zeros((2, surf_here), jnp.float32)
    for iteration in range(COUPLE):
        for substep in range(STEPS):
            padded = with_halo(current, (("sub", 0),), 1)
            current = advance(padded, conduct_slab, velocity_slab, heat_slab, gas_mask)
        flux_field = conduct_slab * (4.0 * current - in_plane(current))
        flat_temp = current.reshape(-1)
        flat_flux = flux_field.reshape(-1)
        export = jnp.stack([flat_temp[surface], flat_flux[surface]])
        group_row = lax.all_gather(export, "sub", axis=1, tiled=True)
        every_row = lax.all_gather(group_row[None], "grp", axis=0, tiled=True)
        source = lax.dynamic_index_in_dim(every_row, partner_row, 0, keepdims=False)
        centre_vals = source[:, centres]
        contrib = (
            jnp.einsum("stk,qsk->qst", patch_mats, centre_vals, precision=lax.Precision.HIGHEST)
            * live_mask[None, :, None]
        )
        partial_rows = jnp.zeros((2, node_total), jnp.float32).at[:, targets].add(contrib)
        interface = lax.psum_scatter(partial_rows, "sub", scatter_dimension=1, tiled=True)
        increment = gain_temp * (interface[0] - export[0]) + gain_flux * interface[1]
        flat_temp = flat_temp.at[surface].add(increment)
        current = flat_temp.reshape(slab_shape)
    return (current.reshape(initial_field.shape), interface[None])


def solution(mesh):
    placed = (
        P("grp", "sub", None),
        P("grp", "sub", None),
        P("grp", "sub", None),
        P("grp", "sub", None),
        P(),
        P(),
        P("grp", "sub"),
        P("grp", None),
        P("grp", "sub", None),
        P("grp", "sub", None),
        P("grp", "sub", None, None),
    )
    return jax.shard_map(
        local,
        mesh=mesh,
        in_specs=placed,
        out_specs=(P("grp", "sub", None), P("grp", None, "sub")),
        check_vma=False,
    )
```

profile of v0, /device:TPU:0, one launch (start us, length us, event | category | flops | bytes accessed | tf_op | source)
XLA Modules:
  0.0 579.5 jit_solution(10298618127133347024)
XLA Ops:
  21.1 5.8 %collective-permute-start.3 = (f32[1,128,128]{2,1,0:T(8,128)S(1)}, f32[1,128,128]{2,1,0:T(8,128)S(1)}, u32[]{:S(2)}, u32[]{:S(2)}) collective-permute-start(f32[1,128,128]{2,1,0:T(8,128)S(1)} %get-tuple-element.197), channel_id=1, source_target_pairs={{0,1},{1,2},{2,3},{3,4},{4,5},{5,6},{6,7},{8,9},{9,10},{10,11},{11... | collective-permute-start | bytes 196616 | tf_op jit(solution)/shard_map/ppermute | solution.py:18
  29.5 4.7 collective-permute-start.5
  36.8 5.3 collective-permute-start.7
  49.9 17.8 %all_gather.24 = f32[2,4096]{1,0:T(2,128)S(1)} all-gather(f32[2,512]{1,0:T(2,128)S(1)} %pad_maximum_fusion.32), channel_id=1, replica_groups=mesh['grp'=4,'sub'=8] {'sub'}, dimensions={1}, use_global_device_ids=true | all-gather | bytes 36864 | tf_op jit(solution)/shard_map/all_gather | solution.py:95
  67.7 8.5 %all-gather.4 = f32[4,2,4096]{2,1,0:T(2,128)S(1)} all-gather(f32[1,2,4096]{2,1,0:T(2,128)S(1)} %bitcast.407), channel_id=2, replica_groups=mesh['grp'=4,'sub'=8] {'grp'}, dimensions={0}, use_global_device_ids=true | all-gather | bytes 163840 | tf_op jit(solution)/shard_map/all_gather | solution.py:96
  78.1 12.4 %gather_fusion.2 = f32[3072,2]{1,0:T(8,128)} fusion(f32[2,4096]{0,1:T(8,128)} %bitcast.398, s32[3072]{0:T(1024)S(1)} %fusion.206), kind=kCustom, calls=%fused_computation.2 | custom fusion | bytes 61440 | tf_op jit(solution)/shard_map/gather | solution.py:98
  96.7 18.6 %scatter_custom_fusion = f32[2,4096]{0,1:T(8,128)} fusion(s32[3072]{0:T(1024)S(1)} %fusion.204, f32[3072,2]{1,0:T(8,128)} %copy.33, f32[]{:T(128)} %constant.47.clone.1), kind=kCustom, calls=%fused_computation.42 | custom fusion | flops 6144 | bytes 33280 | tf_op jit(solution)/shard_map/scatter-add | solution.py:103
  115.4 36.2 %reduce-scatter.5.cloned.1.call-done = f32[2,512]{0,1:T(8,128)} async-done(((f32[2,4096]{0,1:T(8,128)}), f32[2,512]{0,1:T(8,128)}) %reduce-scatter.5.cloned.1.call-update) | async-done | bytes 4112 | tf_op jit(solution)/shard_map/reduce_scatter | solution.py:104
  153.0 3.4 scatter_fusion
  169.2 5.7 collective-permute-start.13
  177.1 5.3 collective-permute-start.15
  190.1 16.6 %all_gather.26 = f32[2,4096]{1,0:T(2,128)S(1)} all-gather(f32[2,512]{1,0:T(2,128)S(1)} %pad_maximum_fusion.33), channel_id=1, replica_groups=mesh['grp'=4,'sub'=8] {'sub'}, dimensions={1}, use_global_device_ids=true | all-gather | bytes 36864 | tf_op jit(solution)/shard_map/all_gather | solution.py:95
  206.7 8.3 %all-gather.5 = f32[4,2,4096]{2,1,0:T(2,128)S(1)} all-gather(f32[1,2,4096]{2,1,0:T(2,128)S(1)} %bitcast.408), channel_id=3, replica_groups=mesh['grp'=4,'sub'=8] {'grp'}, dimensions={0}, use_global_device_ids=true | all-gather | bytes 163840 | tf_op jit(solution)/shard_map/all_gather | solution.py:96
  217.0 12.4 %gather_fusion.5 = f32[3072,2]{1,0:T(8,128)} fusion(f32[2,4096]{0,1:T(8,128)} %bitcast.399, s32[3072]{0:T(1024)S(1)} %fusion.206), kind=kCustom, calls=%fused_computation.5 | custom fusion | bytes 61440 | tf_op jit(solution)/shard_map/gather | solution.py:98
  235.6 18.6 %scatter_custom_fusion.2 = f32[2,4096]{0,1:T(8,128)} fusion(s32[3072]{0:T(1024)S(1)} %fusion.204, f32[3072,2]{1,0:T(8,128)} %copy.36, f32[]{:T(128)} %constant.47.clone.1), kind=kCustom, calls=%fused_computation.40 | custom fusion | flops 6144 | bytes 33280 | tf_op jit(solution)/shard_map/scatter-add | solution.py:103
  254.3 35.6 %reduce-scatter.7.cloned.1.call-done = f32[2,512]{0,1:T(8,128)} async-done(((f32[2,4096]{0,1:T(8,128)}), f32[2,512]{0,1:T(8,128)}) %reduce-scatter.7.cloned.1.call-update) | async-done | bytes 4112 | tf_op jit(solution)/shard_map/reduce_scatter | solution.py:104
  291.3 3.4 scatter_fusion.1
  307.5 5.3 collective-permute-start.21
  315.3 5.3 collective-permute-start.23
  328.4 16.8 %all_gather.28 = f32[2,4096]{1,0:T(2,128)S(1)} all-gather(f32[2,512]{1,0:T(2,128)S(1)} %pad_maximum_fusion.34), channel_id=1, replica_groups=mesh['grp'=4,'sub'=8] {'sub'}, dimensions={1}, use_global_device_ids=true | all-gather | bytes 36864 | tf_op jit(solution)/shard_map/all_gather | solution.py:95
  345.2 8.4 %all-gather.6 = f32[4,2,4096]{2,1,0:T(2,128)S(1)} all-gather(f32[1,2,4096]{2,1,0:T(2,128)S(1)} %bitcast.409), channel_id=4, replica_groups=mesh['grp'=4,'sub'=8] {'grp'}, dimensions={0}, use_global_device_ids=true | all-gather | bytes 163840 | tf_op jit(solution)/shard_map/all_gather | solution.py:96
  355.6 12.4 %gather_fusion.8 = f32[3072,2]{1,0:T(8,128)} fusion(f32[2,4096]{0,1:T(8,128)} %bitcast.400, s32[3072]{0:T(1024)S(1)} %fusion.206), kind=kCustom, calls=%fused_computation.8 | custom fusion | bytes 61440 | tf_op jit(solution)/shard_map/gather | solution.py:98
  374.1 18.6 %scatter_custom_fusion.4 = f32[2,4096]{0,1:T(8,128)} fusion(s32[3072]{0:T(1024)S(1)} %fusion.204, f32[3072,2]{1,0:T(8,128)} %copy.39, f32[]{:T(128)} %constant.47.clone.1), kind=kCustom, calls=%fused_computation.38 | custom fusion | flops 6144 | bytes 33280 | tf_op jit(solution)/shard_map/scatter-add | solution.py:103
  392.8 35.4 %reduce-scatter.9.cloned.1.call-done = f32[2,512]{0,1:T(8,128)} async-done(((f32[2,4096]{0,1:T(8,128)}), f32[2,512]{0,1:T(8,128)}) %reduce-scatter.9.cloned.1.call-update) | async-done | bytes 4112 | tf_op jit(solution)/shard_map/reduce_scatter | solution.py:104
  429.5 3.4 scatter_fusion.2
  445.8 5.3 collective-permute-start.29
  453.6 5.3 collective-permute-start.31
  466.7 16.6 %all_gather.30 = f32[2,4096]{1,0:T(2,128)S(1)} all-gather(f32[2,512]{1,0:T(2,128)S(1)} %pad_maximum_fusion.35), channel_id=1, replica_groups=mesh['grp'=4,'sub'=8] {'sub'}, dimensions={1}, use_global_device_ids=true | all-gather | bytes 36864 | tf_op jit(solution)/shard_map/all_gather | solution.py:95
  483.3 8.6 %all-gather.7 = f32[4,2,4096]{2,1,0:T(2,128)S(1)} all-gather(f32[1,2,4096]{2,1,0:T(2,128)S(1)} %bitcast.410), channel_id=5, replica_groups=mesh['grp'=4,'sub'=8] {'grp'}, dimensions={0}, use_global_device_ids=true | all-gather | bytes 163840 | tf_op jit(solution)/shard_map/all_gather | solution.py:96
  493.9 12.4 %gather_fusion.11 = f32[3072,2]{1,0:T(8,128)} fusion(f32[2,4096]{0,1:T(8,128)} %bitcast.397, s32[3072]{0:T(1024)S(1)} %fusion.206), kind=kCustom, calls=%fused_computation.11 | custom fusion | bytes 61440 | tf_op jit(solution)/shard_map/gather | solution.py:98
  512.5 18.6 %scatter_custom_fusion.6 = f32[2,4096]{0,1:T(8,128)} fusion(s32[3072]{0:T(1024)S(1)} %fusion.204, f32[3072,2]{1,0:T(8,128)} %copy.42, f32[]{:T(128)} %constant.47.clone.1), kind=kCustom, calls=%fused_computation.36 | custom fusion | flops 6144 | bytes 33280 | tf_op jit(solution)/shard_map/scatter-add | solution.py:103
  531.1 35.4 %reduce-scatter.11.cloned.1.call-done = f32[2,512]{0,1:T(8,128)} async-done(((f32[2,4096]{0,1:T(8,128)}), f32[2,512]{0,1:T(8,128)}) %reduce-scatter.11.cloned.1.call-update) | async-done | bytes 4112 | tf_op jit(solution)/shard_map/reduce_scatter | solution.py:104
  (252 shorter events, 134.6 us)
Async XLA Ops:
  7.3 144.4 %reduce-scatter.5.cloned.1.call-start = ((), (), s32[]{:S(2)}) async-start(), calls=%async_computation.4 | async-start | bytes 2359296 | tf_op jit(solution)/shard_map/reduce_scatter | solution.py:104
  8.6 10.8 %collective-permute-start.1 = (f32[1,128,128]{2,1,0:T(8,128)S(1)}, f32[1,128,128]{2,1,0:T(8,128)S(1)}, u32[]{:S(2)}, u32[]{:S(2)}) collective-permute-start(f32[1,128,128]{2,1,0:T(8,128)S(1)} %bitcast.417), channel_id=1, source_target_pairs={{0,1},{1,2},{2,3},{3,4},{4,5},{5,6},{6,7},{8,9},{9,10},{10,11},{11... | collective-permute-start | bytes 196616 | tf_op jit(solution)/shard_map/ppermute | solution.py:18
  11.0 8.4 %collective-permute-start = (f32[1,128,128]{2,1,0:T(8,128)S(1)}, f32[1,128,128]{2,1,0:T(8,128)S(1)}, u32[]{:S(2)}, u32[]{:S(2)}) collective-permute-start(f32[1,128,128]{2,1,0:T(8,128)S(1)} %bitcast.416), channel_id=1, source_target_pairs={{1,0},{2,1},{3,2},{4,3},{5,4},{6,5},{7,6},{9,8},{10,9},{11,10},{12... | collective-permute-start | bytes 196616 | tf_op jit(solution)/shard_map/ppermute | solution.py:20
  19.8 7.2 %collective-permute-start.2 = (f32[1,128,128]{2,1,0:T(8,128)S(1)}, f32[1,128,128]{2,1,0:T(8,128)S(1)}, u32[]{:S(2)}, u32[]{:S(2)}) collective-permute-start(f32[1,128,128]{2,1,0:T(8,128)S(1)} %get-tuple-element.196), channel_id=1, source_target_pairs={{1,0},{2,1},{3,2},{4,3},{5,4},{6,5},{7,6},{9,8},{10,9},{11,10},{12... | collective-permute-start | bytes 196616 | tf_op jit(solution)/shard_map/ppermute | solution.py:20
  21.1 6.7 %collective-permute-start.3 = (f32[1,128,128]{2,1,0:T(8,128)S(1)}, f32[1,128,128]{2,1,0:T(8,128)S(1)}, u32[]{:S(2)}, u32[]{:S(2)}) collective-permute-start(f32[1,128,128]{2,1,0:T(8,128)S(1)} %get-tuple-element.197), channel_id=1, source_target_pairs={{0,1},{1,2},{2,3},{3,4},{4,5},{5,6},{6,7},{8,9},{9,10},{10,11},{11... | collective-permute-start | bytes 196616 | tf_op jit(solution)/shard_map/ppermute | solution.py:18
  28.2 6.0 %collective-permute-start.4 = (f32[1,128,128]{2,1,0:T(8,128)S(1)}, f32[1,128,128]{2,1,0:T(8,128)S(1)}, u32[]{:S(2)}, u32[]{:S(2)}) collective-permute-start(f32[1,128,128]{2,1,0:T(8,128)S(1)} %get-tuple-element.186), channel_id=1, source_target_pairs={{1,0},{2,1},{3,2},{4,3},{5,4},{6,5},{7,6},{9,8},{10,9},{11,10},{12... | collective-permute-start | bytes 196616 | tf_op jit(solution)/shard_map/ppermute | solution.py:20
  29.5 5.6 collective-permute-start.5
  35.5 6.6 %collective-permute-start.6 = (f32[1,128,128]{2,1,0:T(8,128)S(1)}, f32[1,128,128]{2,1,0:T(8,128)S(1)}, u32[]{:S(2)}, u32[]{:S(2)}) collective-permute-start(f32[1,128,128]{2,1,0:T(8,128)S(1)} %get-tuple-element.176), channel_id=1, source_target_pairs={{1,0},{2,1},{3,2},{4,3},{5,4},{6,5},{7,6},{9,8},{10,9},{11,10},{12... | collective-permute-start | bytes 196616 | tf_op jit(solution)/shard_map/ppermute | solution.py:20
  36.8 6.2 %collective-permute-start.7 = (f32[1,128,128]{2,1,0:T(8,128)S(1)}, f32[1,128,128]{2,1,0:T(8,128)S(1)}, u32[]{:S(2)}, u32[]{:S(2)}) collective-permute-start(f32[1,128,128]{2,1,0:T(8,128)S(1)} %get-tuple-element.177), channel_id=1, source_target_pairs={{0,1},{1,2},{2,3},{3,4},{4,5},{5,6},{6,7},{8,9},{9,10},{10,11},{11... | collective-permute-start | bytes 196616 | tf_op jit(solution)/shard_map/ppermute | solution.py:18
  115.3 174.6 %reduce-scatter.7.cloned.1.call-start = ((), (), s32[]{:S(2)}) async-start(), calls=%async_computation.5 | async-start | bytes 2359296 | tf_op jit(solution)/shard_map/reduce_scatter | solution.py:104
  156.6 4.4 collective-permute-start.8
  157.9 3.9 collective-permute-start.9
  162.3 4.4 collective-permute-start.10
  163.6 3.9 collective-permute-start.11
  167.9 7.1 %collective-permute-start.12 = (f32[1,128,128]{2,1,0:T(8,128)S(1)}, f32[1,128,128]{2,1,0:T(8,128)S(1)}, u32[]{:S(2)}, u32[]{:S(2)}) collective-permute-start(f32[1,128,128]{2,1,0:T(8,128)S(1)} %get-tuple-element.138), channel_id=1, source_target_pairs={{1,0},{2,1},{3,2},{4,3},{5,4},{6,5},{7,6},{9,8},{10,9},{11,10},{12... | collective-permute-start | bytes 196616 | tf_op jit(solution)/shard_map/ppermute | solution.py:20
  169.2 6.2 %collective-permute-start.13 = (f32[1,128,128]{2,1,0:T(8,128)S(1)}, f32[1,128,128]{2,1,0:T(8,128)S(1)}, u32[]{:S(2)}, u32[]{:S(2)}) collective-permute-start(f32[1,128,128]{2,1,0:T(8,128)S(1)} %get-tuple-element.139), channel_id=1, source_target_pairs={{0,1},{1,2},{2,3},{3,4},{4,5},{5,6},{6,7},{8,9},{9,10},{10,11},{11... | collective-permute-start | bytes 196616 | tf_op jit(solution)/shard_map/ppermute | solution.py:18
  175.8 6.6 %collective-permute-start.14 = (f32[1,128,128]{2,1,0:T(8,128)S(1)}, f32[1,128,128]{2,1,0:T(8,128)S(1)}, u32[]{:S(2)}, u32[]{:S(2)}) collective-permute-start(f32[1,128,128]{2,1,0:T(8,128)S(1)} %get-tuple-element.128), channel_id=1, source_target_pairs={{1,0},{2,1},{3,2},{4,3},{5,4},{6,5},{7,6},{9,8},{10,9},{11,10},{12... | collective-permute-start | bytes 196616 | tf_op jit(solution)/shard_map/ppermute | solution.py:20
  177.1 6.2 %collective-permute-start.15 = (f32[1,128,128]{2,1,0:T(8,128)S(1)}, f32[1,128,128]{2,1,0:T(8,128)S(1)}, u32[]{:S(2)}, u32[]{:S(2)}) collective-permute-start(f32[1,128,128]{2,1,0:T(8,128)S(1)} %get-tuple-element.129), channel_id=1, source_target_pairs={{0,1},{1,2},{2,3},{3,4},{4,5},{5,6},{6,7},{8,9},{9,10},{10,11},{11... | collective-permute-start | bytes 196616 | tf_op jit(solution)/shard_map/ppermute | solution.py:18
  254.3 173.9 %reduce-scatter.9.cloned.1.call-start = ((), (), s32[]{:S(2)}) async-start(), calls=%async_computation.6 | async-start | bytes 2359296 | tf_op jit(solution)/shard_map/reduce_scatter | solution.py:104
  294.9 4.4 collective-permute-start.16
  300.6 4.4 collective-permute-start.18
  306.2 6.6 %collective-permute-start.20 = (f32[1,128,128]{2,1,0:T(8,128)S(1)}, f32[1,128,128]{2,1,0:T(8,128)S(1)}, u32[]{:S(2)}, u32[]{:S(2)}) collective-permute-start(f32[1,128,128]{2,1,0:T(8,128)S(1)} %get-tuple-element.90), channel_id=1, source_target_pairs={{1,0},{2,1},{3,2},{4,3},{5,4},{6,5},{7,6},{9,8},{10,9},{11,10},{12... | collective-permute-start | bytes 196616 | tf_op jit(solution)/shard_map/ppermute | solution.py:20
  307.5 6.2 %collective-permute-start.21 = (f32[1,128,128]{2,1,0:T(8,128)S(1)}, f32[1,128,128]{2,1,0:T(8,128)S(1)}, u32[]{:S(2)}, u32[]{:S(2)}) collective-permute-start(f32[1,128,128]{2,1,0:T(8,128)S(1)} %get-tuple-element.91), channel_id=1, source_target_pairs={{0,1},{1,2},{2,3},{3,4},{4,5},{5,6},{6,7},{8,9},{9,10},{10,11},{11... | collective-permute-start | bytes 196616 | tf_op jit(solution)/shard_map/ppermute | solution.py:18
  314.0 6.6 %collective-permute-start.22 = (f32[1,128,128]{2,1,0:T(8,128)S(1)}, f32[1,128,128]{2,1,0:T(8,128)S(1)}, u32[]{:S(2)}, u32[]{:S(2)}) collective-permute-start(f32[1,128,128]{2,1,0:T(8,128)S(1)} %get-tuple-element.80), channel_id=1, source_target_pairs={{1,0},{2,1},{3,2},{4,3},{5,4},{6,5},{7,6},{9,8},{10,9},{11,10},{12... | collective-permute-start | bytes 196616 | tf_op jit(solution)/shard_map/ppermute | solution.py:20
  315.3 6.2 %collective-permute-start.23 = (f32[1,128,128]{2,1,0:T(8,128)S(1)}, f32[1,128,128]{2,1,0:T(8,128)S(1)}, u32[]{:S(2)}, u32[]{:S(2)}) collective-permute-start(f32[1,128,128]{2,1,0:T(8,128)S(1)} %get-tuple-element.81), channel_id=1, source_target_pairs={{0,1},{1,2},{2,3},{3,4},{4,5},{5,6},{6,7},{8,9},{9,10},{10,11},{11... | collective-permute-start | bytes 196616 | tf_op jit(solution)/shard_map/ppermute | solution.py:18
  392.8 173.7 %reduce-scatter.11.cloned.1.call-start = ((), (), s32[]{:S(2)}) async-start(), calls=%async_computation.7 | async-start | bytes 2359296 | tf_op jit(solution)/shard_map/reduce_scatter | solution.py:104
  433.2 4.4 collective-permute-start.24
  438.8 4.4 collective-permute-start.26
  444.5 6.6 %collective-permute-start.28 = (f32[1,128,128]{2,1,0:T(8,128)S(1)}, f32[1,128,128]{2,1,0:T(8,128)S(1)}, u32[]{:S(2)}, u32[]{:S(2)}) collective-permute-start(f32[1,128,128]{2,1,0:T(8,128)S(1)} %get-tuple-element.42), channel_id=1, source_target_pairs={{1,0},{2,1},{3,2},{4,3},{5,4},{6,5},{7,6},{9,8},{10,9},{11,10},{12... | collective-permute-start | bytes 196616 | tf_op jit(solution)/shard_map/ppermute | solution.py:20
  445.8 6.2 %collective-permute-start.29 = (f32[1,128,128]{2,1,0:T(8,128)S(1)}, f32[1,128,128]{2,1,0:T(8,128)S(1)}, u32[]{:S(2)}, u32[]{:S(2)}) collective-permute-start(f32[1,128,128]{2,1,0:T(8,128)S(1)} %get-tuple-element.43), channel_id=1, source_target_pairs={{0,1},{1,2},{2,3},{3,4},{4,5},{5,6},{6,7},{8,9},{9,10},{10,11},{11... | collective-permute-start | bytes 196616 | tf_op jit(solution)/shard_map/ppermute | solution.py:18
  452.3 6.6 %collective-permute-start.30 = (f32[1,128,128]{2,1,0:T(8,128)S(1)}, f32[1,128,128]{2,1,0:T(8,128)S(1)}, u32[]{:S(2)}, u32[]{:S(2)}) collective-permute-start(f32[1,128,128]{2,1,0:T(8,128)S(1)} %get-tuple-element.32), channel_id=1, source_target_pairs={{1,0},{2,1},{3,2},{4,3},{5,4},{6,5},{7,6},{9,8},{10,9},{11,10},{12... | collective-permute-start | bytes 196616 | tf_op jit(solution)/shard_map/ppermute | solution.py:20
  453.6 6.2 %collective-permute-start.31 = (f32[1,128,128]{2,1,0:T(8,128)S(1)}, f32[1,128,128]{2,1,0:T(8,128)S(1)}, u32[]{:S(2)}, u32[]{:S(2)}) collective-permute-start(f32[1,128,128]{2,1,0:T(8,128)S(1)} %get-tuple-element.33), channel_id=1, source_target_pairs={{0,1},{1,2},{2,3},{3,4},{4,5},{5,6},{6,7},{8,9},{9,10},{10,11},{11... | collective-permute-start | bytes 196616 | tf_op jit(solution)/shard_map/ppermute | solution.py:18
  (14 other events, 189.1 us)
Sparse Core Ops, SparseCore 0:
  115.4 36.1 reduce-scatter.4
  254.4 35.4 reduce-scatter.6
  392.9 35.2 reduce-scatter.8
  531.2 35.2 reduce-scatter.10
where the time goes:
time: 589 us; the launch traced here: 580 us
  waiting for transfers between devices  155 us (26%)
  local copies, waits for them, and re-layouts  108 us (18%)
  blocking collectives  102 us (17%)
  other arithmetic  97.4 us (17%)
  starting transfers between devices  89.5 us (15%)
  between operations  18.2 us (3%)
  matrix products  10.2 us (2%)
    reduce_scatter x4, waiting for transfers between devices, local(): lax.psum_scatter(partial_rows, 'sub', scatter_dimension=1, tiled=True)  143 us
    scatter-add x4, other arithmetic, local(): jnp.zeros((2, node_total), jnp.float32).at[:, targets].add(contrib)  74.5 us
    ppermute x16, starting transfers between devices, with_halo(): lax.ppermute(tail, axis, [(i, (i + 1) % count) for i in range(ends)])  68.7 us
    all_gather x4, blocking collectives, local(): group_row = lax.all_gather(export, 'sub', axis=1, tiled=True)  67.7 us
    gather x8, local copies, waits for them, and re-layouts, local(): centre_vals = source[:, centres]  57.2 us
    all_gather x4, blocking collectives, local(): every_row = lax.all_gather(group_row[None], 'grp', axis=0, tiled=True)  33.8 us
    gather x8, local copies, waits for them, and re-layouts, local(): export = jnp.stack([flat_temp[surface], flat_flux[surface]])  25.1 us
    ppermute x16, starting transfers between devices, with_halo(): lax.ppermute(head, axis, [((i + 1) % count, i) for i in range(ends)])  20.7 us
  transfers between devices with their start and end apart: 36, of which 19 were waited for; matrix products, arithmetic and copies ran while one was open for 1% of the time, Pallas kernels for 0%

commit v1 on v0

--- a/solution.py
+++ b/solution.py
@@ -92,7 +92,7 @@
         flat_temp = current.reshape(-1)
         flat_flux = flux_field.reshape(-1)
         export = jnp.stack([flat_temp[surface], flat_flux[surface]])
-        group_row = lax.all_gather(export, "sub", axis=1, tiled=True)
+        group_row = jnp.concatenate(lax.all_gather(export, "sub"), axis=1)
         every_row = lax.all_gather(group_row[None], "grp", axis=0, tiled=True)
         source = lax.dynamic_index_in_dim(every_row, partner_row, 0, keepdims=False)
         centre_vals = source[:, centres]

time: 589 us -> 589 us (level)
  no operation moved by 1% of the time
where the time goes in v1:
time: 589 us; the launch traced here: 580 us
  waiting for transfers between devices  155 us (26%)
  local copies, waits for them, and re-layouts  108 us (18%)
  blocking collectives  102 us (17%)
  other arithmetic  97.4 us (17%)
  starting transfers between devices  89.5 us (15%)
  between operations  18.2 us (3%)
  matrix products  10.2 us (2%)
    reduce_scatter x4, waiting for transfers between devices, local(): lax.psum_scatter(partial_rows, 'sub', scatter_dimension=1, tiled=True)  143 us
    scatter-add x4, other arithmetic, local(): jnp.zeros((2, node_total), jnp.float32).at[:, targets].add(contrib)  74.5 us
    ppermute x16, starting transfers between devices, with_halo(): lax.ppermute(tail, axis, [(i, (i + 1) % count) for i in range(ends)])  68.7 us
    all_gather x4, blocking collectives, local(): group_row = jnp.concatenate(lax.all_gather(export, 'sub'), axis=1)  67.7 us
    gather x8, local copies, waits for them, and re-layouts, local(): centre_vals = source[:, centres]  57.2 us
    all_gather x4, blocking collectives, local(): every_row = lax.all_gather(group_row[None], 'grp', axis=0, tiled=True)  33.8 us
    gather x8, local copies, waits for them, and re-layouts, local(): export = jnp.stack([flat_temp[surface], flat_flux[surface]])  25.1 us
    ppermute x16, starting transfers between devices, with_halo(): lax.ppermute(head, axis, [((i + 1) % count, i) for i in range(ends)])  20.7 us
  transfers between devices with their start and end apart: 36, of which 19 were waited for; matrix products, arithmetic and copies ran while one was open for 1% of the time, Pallas kernels for 0%

profile of v1, /device:TPU:0, one launch (start us, length us, event | category | flops | bytes accessed | tf_op | source)
XLA Modules:
  0.0 579.5 jit_solution(7293044574122859886)
XLA Ops:
  21.1 5.8 %collective-permute-start.3 = (f32[1,128,128]{2,1,0:T(8,128)S(1)}, f32[1,128,128]{2,1,0:T(8,128)S(1)}, u32[]{:S(2)}, u32[]{:S(2)}) collective-permute-start(f32[1,128,128]{2,1,0:T(8,128)S(1)} %get-tuple-element.199), channel_id=1, source_target_pairs={{0,1},{1,2},{2,3},{3,4},{4,5},{5,6},{6,7},{8,9},{9,10},{10,11},{11... | collective-permute-start | bytes 196616 | tf_op jit(solution)/shard_map/ppermute | solution.py:18
  29.5 4.7 collective-permute-start.5
  36.8 5.3 collective-permute-start.7
  49.9 17.8 %all-gather.4 = f32[8,2,512]{2,1,0:T(2,128)S(1)} all-gather(f32[1,2,512]{2,1,0:T(2,128)S(1)} %maximum_bitcast_fusion), channel_id=2, replica_groups=mesh['grp'=4,'sub'=8] {'sub'}, dimensions={0}, use_global_device_ids=true | all-gather | bytes 36864 | tf_op jit(solution)/shard_map/all_gather | solution.py:95
  67.7 8.5 %all_gather.38 = f32[4,2,4096]{2,1,0:T(2,128)S(1)} all-gather(f32[1,2,4096]{2,1,0:T(2,128)S(1)} %bitcast.423), channel_id=1, replica_groups=mesh['grp'=4,'sub'=8] {'grp'}, dimensions={0}, use_global_device_ids=true | all-gather | bytes 163840 | tf_op jit(solution)/shard_map/all_gather | solution.py:96
  78.1 12.4 %gather_fusion.2 = f32[3072,2]{1,0:T(8,128)} fusion(f32[2,4096]{0,1:T(8,128)} %bitcast.414, s32[3072]{0:T(1024)S(1)} %fusion.206), kind=kCustom, calls=%fused_computation.2 | custom fusion | bytes 61440 | tf_op jit(solution)/shard_map/gather | solution.py:98
  96.7 18.6 %scatter_custom_fusion = f32[2,4096]{0,1:T(8,128)} fusion(s32[3072]{0:T(1024)S(1)} %fusion.204, f32[3072,2]{1,0:T(8,128)} %copy.42, f32[]{:T(128)} %constant.47.clone.1), kind=kCustom, calls=%fused_computation.42 | custom fusion | flops 6144 | bytes 33280 | tf_op jit(solution)/shard_map/scatter-add | solution.py:103
  115.4 36.2 %reduce-scatter.5.cloned.1.call-done = f32[2,512]{0,1:T(8,128)} async-done(((f32[2,4096]{0,1:T(8,128)}), f32[2,512]{0,1:T(8,128)}) %reduce-scatter.5.cloned.1.call-update) | async-done | bytes 4112 | tf_op jit(solution)/shard_map/reduce_scatter | solution.py:104
  153.0 3.4 scatter_fusion
  169.2 5.7 collective-permute-start.13
  177.1 5.3 collective-permute-start.15
  190.1 16.6 %all-gather.5 = f32[8,2,512]{2,1,0:T(2,128)S(1)} all-gather(f32[1,2,512]{2,1,0:T(2,128)S(1)} %maximum_bitcast_fusion.1), channel_id=3, replica_groups=mesh['grp'=4,'sub'=8] {'sub'}, dimensions={0}, use_global_device_ids=true | all-gather | bytes 36864 | tf_op jit(solution)/shard_map/all_gather | solution.py:95
  206.7 8.3 %all_gather.41 = f32[4,2,4096]{2,1,0:T(2,128)S(1)} all-gather(f32[1,2,4096]{2,1,0:T(2,128)S(1)} %bitcast.424), channel_id=1, replica_groups=mesh['grp'=4,'sub'=8] {'grp'}, dimensions={0}, use_global_device_ids=true | all-gather | bytes 163840 | tf_op jit(solution)/shard_map/all_gather | solution.py:96
  217.0 12.4 %gather_fusion.5 = f32[3072,2]{1,0:T(8,128)} fusion(f32[2,4096]{0,1:T(8,128)} %bitcast.415, s32[3072]{0:T(1024)S(1)} %fusion.206), kind=kCustom, calls=%fused_computation.5 | custom fusion | bytes 61440 | tf_op jit(solution)/shard_map/gather | solution.py:98
  235.6 18.6 %scatter_custom_fusion.2 = f32[2,4096]{0,1:T(8,128)} fusion(s32[3072]{0:T(1024)S(1)} %fusion.204, f32[3072,2]{1,0:T(8,128)} %copy.45, f32[]{:T(128)} %constant.47.clone.1), kind=kCustom, calls=%fused_computation.40 | custom fusion | flops 6144 | bytes 33280 | tf_op jit(solution)/shard_map/scatter-add | solution.py:103
  254.3 35.6 %reduce-scatter.7.cloned.1.call-done = f32[2,512]{0,1:T(8,128)} async-done(((f32[2,4096]{0,1:T(8,128)}), f32[2,512]{0,1:T(8,128)}) %reduce-scatter.7.cloned.1.call-update) | async-done | bytes 4112 | tf_op jit(solution)/shard_map/reduce_scatter | solution.py:104
  291.3 3.4 scatter_fusion.1
  307.5 5.3 collective-permute-start.21
  315.3 5.3 collective-permute-start.23
  328.4 16.8 %all-gather.6 = f32[8,2,512]{2,1,0:T(2,128)S(1)} all-gather(f32[1,2,512]{2,1,0:T(2,128)S(1)} %maximum_bitcast_fusion.2), channel_id=4, replica_groups=mesh['grp'=4,'sub'=8] {'sub'}, dimensions={0}, use_global_device_ids=true | all-gather | bytes 36864 | tf_op jit(solution)/shard_map/all_gather | solution.py:95
  345.2 8.4 %all_gather.44 = f32[4,2,4096]{2,1,0:T(2,128)S(1)} all-gather(f32[1,2,4096]{2,1,0:T(2,128)S(1)} %bitcast.425), channel_id=1, replica_groups=mesh['grp'=4,'sub'=8] {'grp'}, dimensions={0}, use_global_device_ids=true | all-gather | bytes 163840 | tf_op jit(solution)/shard_map/all_gather | solution.py:96
  355.6 12.4 %gather_fusion.8 = f32[3072,2]{1,0:T(8,128)} fusion(f32[2,4096]{0,1:T(8,128)} %bitcast.416, s32[3072]{0:T(1024)S(1)} %fusion.206), kind=kCustom, calls=%fused_computation.8 | custom fusion | bytes 61440 | tf_op jit(solution)/shard_map/gather | solution.py:98
  374.1 18.6 %scatter_custom_fusion.4 = f32[2,4096]{0,1:T(8,128)} fusion(s32[3072]{0:T(1024)S(1)} %fusion.204, f32[3072,2]{1,0:T(8,128)} %copy.48, f32[]{:T(128)} %constant.47.clone.1), kind=kCustom, calls=%fused_computation.38 | custom fusion | flops 6144 | bytes 33280 | tf_op jit(solution)/shard_map/scatter-add | solution.py:103
  392.8 35.4 %reduce-scatter.9.cloned.1.call-done = f32[2,512]{0,1:T(8,128)} async-done(((f32[2,4096]{0,1:T(8,128)}), f32[2,512]{0,1:T(8,128)}) %reduce-scatter.9.cloned.1.call-update) | async-done | bytes 4112 | tf_op jit(solution)/shard_map/reduce_scatter | solution.py:104
  429.5 3.4 scatter_fusion.2
  445.8 5.3 collective-permute-start.29
  453.6 5.3 collective-permute-start.31
  466.7 16.6 %all-gather.7 = f32[8,2,512]{2,1,0:T(2,128)S(1)} all-gather(f32[1,2,512]{2,1,0:T(2,128)S(1)} %maximum_bitcast_fusion.3), channel_id=5, replica_groups=mesh['grp'=4,'sub'=8] {'sub'}, dimensions={0}, use_global_device_ids=true | all-gather | bytes 36864 | tf_op jit(solution)/shard_map/all_gather | solution.py:95
  483.3 8.6 %all_gather.47 = f32[4,2,4096]{2,1,0:T(2,128)S(1)} all-gather(f32[1,2,4096]{2,1,0:T(2,128)S(1)} %bitcast.426), channel_id=1, replica_groups=mesh['grp'=4,'sub'=8] {'grp'}, dimensions={0}, use_global_device_ids=true | all-gather | bytes 163840 | tf_op jit(solution)/shard_map/all_gather | solution.py:96
  493.9 12.4 %gather_fusion.11 = f32[3072,2]{1,0:T(8,128)} fusion(f32[2,4096]{0,1:T(8,128)} %bitcast.413, s32[3072]{0:T(1024)S(1)} %fusion.206), kind=kCustom, calls=%fused_computation.11 | custom fusion | bytes 61440 | tf_op jit(solution)/shard_map/gather | solution.py:98
  512.5 18.6 %scatter_custom_fusion.6 = f32[2,4096]{0,1:T(8,128)} fusion(s32[3072]{0:T(1024)S(1)} %fusion.204, f32[3072,2]{1,0:T(8,128)} %copy.51, f32[]{:T(128)} %constant.47.clone.1), kind=kCustom, calls=%fused_computation.36 | custom fusion | flops 6144 | bytes 33280 | tf_op jit(solution)/shard_map/scatter-add | solution.py:103
  531.1 35.4 %reduce-scatter.11.cloned.1.call-done = f32[2,512]{0,1:T(8,128)} async-done(((f32[2,4096]{0,1:T(8,128)}), f32[2,512]{0,1:T(8,128)}) %reduce-scatter.11.cloned.1.call-update) | async-done | bytes 4112 | tf_op jit(solution)/shard_map/reduce_scatter | solution.py:104
  (252 shorter events, 134.6 us)
Async XLA Ops:
  7.3 144.4 %reduce-scatter.5.cloned.1.call-start = ((), (), s32[]{:S(2)}) async-start(), calls=%async_computation.4 | async-start | bytes 2359296 | tf_op jit(solution)/shard_map/reduce_scatter | solution.py:104
  8.6 10.8 %collective-permute-start.1 = (f32[1,128,128]{2,1,0:T(8,128)S(1)}, f32[1,128,128]{2,1,0:T(8,128)S(1)}, u32[]{:S(2)}, u32[]{:S(2)}) collective-permute-start(f32[1,128,128]{2,1,0:T(8,128)S(1)} %bitcast.433), channel_id=1, source_target_pairs={{0,1},{1,2},{2,3},{3,4},{4,5},{5,6},{6,7},{8,9},{9,10},{10,11},{11... | collective-permute-start | bytes 196616 | tf_op jit(solution)/shard_map/ppermute | solution.py:18
  11.0 8.4 %collective-permute-start = (f32[1,128,128]{2,1,0:T(8,128)S(1)}, f32[1,128,128]{2,1,0:T(8,128)S(1)}, u32[]{:S(2)}, u32[]{:S(2)}) collective-permute-start(f32[1,128,128]{2,1,0:T(8,128)S(1)} %bitcast.432), channel_id=1, source_target_pairs={{1,0},{2,1},{3,2},{4,3},{5,4},{6,5},{7,6},{9,8},{10,9},{11,10},{12... | collective-permute-start | bytes 196616 | tf_op jit(solution)/shard_map/ppermute | solution.py:20
  19.8 7.2 %collective-permute-start.2 = (f32[1,128,128]{2,1,0:T(8,128)S(1)}, f32[1,128,128]{2,1,0:T(8,128)S(1)}, u32[]{:S(2)}, u32[]{:S(2)}) collective-permute-start(f32[1,128,128]{2,1,0:T(8,128)S(1)} %get-tuple-element.198), channel_id=1, source_target_pairs={{1,0},{2,1},{3,2},{4,3},{5,4},{6,5},{7,6},{9,8},{10,9},{11,10},{12... | collective-permute-start | bytes 196616 | tf_op jit(solution)/shard_map/ppermute | solution.py:20
  21.1 6.7 %collective-permute-start.3 = (f32[1,128,128]{2,1,0:T(8,128)S(1)}, f32[1,128,128]{2,1,0:T(8,128)S(1)}, u32[]{:S(2)}, u32[]{:S(2)}) collective-permute-start(f32[1,128,128]{2,1,0:T(8,128)S(1)} %get-tuple-element.199), channel_id=1, source_target_pairs={{0,1},{1,2},{2,3},{3,4},{4,5},{5,6},{6,7},{8,9},{9,10},{10,11},{11... | collective-permute-start | bytes 196616 | tf_op jit(solution)/shard_map/ppermute | solution.py:18
  28.2 6.0 %collective-permute-start.4 = (f32[1,128,128]{2,1,0:T(8,128)S(1)}, f32[1,128,128]{2,1,0:T(8,128)S(1)}, u32[]{:S(2)}, u32[]{:S(2)}) collective-permute-start(f32[1,128,128]{2,1,0:T(8,128)S(1)} %get-tuple-element.188), channel_id=1, source_target_pairs={{1,0},{2,1},{3,2},{4,3},{5,4},{6,5},{7,6},{9,8},{10,9},{11,10},{12... | collective-permute-start | bytes 196616 | tf_op jit(solution)/shard_map/ppermute | solution.py:20
  29.5 5.6 collective-permute-start.5
  35.5 6.6 %collective-permute-start.6 = (f32[1,128,128]{2,1,0:T(8,128)S(1)}, f32[1,128,128]{2,1,0:T(8,128)S(1)}, u32[]{:S(2)}, u32[]{:S(2)}) collective-permute-start(f32[1,128,128]{2,1,0:T(8,128)S(1)} %get-tuple-element.178), channel_id=1, source_target_pairs={{1,0},{2,1},{3,2},{4,3},{5,4},{6,5},{7,6},{9,8},{10,9},{11,10},{12... | collective-permute-start | bytes 196616 | tf_op jit(solution)/shard_map/ppermute | solution.py:20
  36.8 6.2 %collective-permute-start.7 = (f32[1,128,128]{2,1,0:T(8,128)S(1)}, f32[1,128,128]{2,1,0:T(8,128)S(1)}, u32[]{:S(2)}, u32[]{:S(2)}) collective-permute-start(f32[1,128,128]{2,1,0:T(8,128)S(1)} %get-tuple-element.179), channel_id=1, source_target_pairs={{0,1},{1,2},{2,3},{3,4},{4,5},{5,6},{6,7},{8,9},{9,10},{10,11},{11... | collective-permute-start | bytes 196616 | tf_op jit(solution)/shard_map/ppermute | solution.py:18
  115.3 174.6 %reduce-scatter.7.cloned.1.call-start = ((), (), s32[]{:S(2)}) async-start(), calls=%async_computation.5 | async-start | bytes 2359296 | tf_op jit(solution)/shard_map/reduce_scatter | solution.py:104
  156.6 4.4 collective-permute-start.8
  157.9 3.9 collective-permute-start.9
  162.3 4.4 collective-permute-start.10
  163.6 3.9 collective-permute-start.11
  167.9 7.1 %collective-permute-start.12 = (f32[1,128,128]{2,1,0:T(8,128)S(1)}, f32[1,128,128]{2,1,0:T(8,128)S(1)}, u32[]{:S(2)}, u32[]{:S(2)}) collective-permute-start(f32[1,128,128]{2,1,0:T(8,128)S(1)} %get-tuple-element.140), channel_id=1, source_target_pairs={{1,0},{2,1},{3,2},{4,3},{5,4},{6,5},{7,6},{9,8},{10,9},{11,10},{12... | collective-permute-start | bytes 196616 | tf_op jit(solution)/shard_map/ppermute | solution.py:20
  169.2 6.2 %collective-permute-start.13 = (f32[1,128,128]{2,1,0:T(8,128)S(1)}, f32[1,128,128]{2,1,0:T(8,128)S(1)}, u32[]{:S(2)}, u32[]{:S(2)}) collective-permute-start(f32[1,128,128]{2,1,0:T(8,128)S(1)} %get-tuple-element.141), channel_id=1, source_target_pairs={{0,1},{1,2},{2,3},{3,4},{4,5},{5,6},{6,7},{8,9},{9,10},{10,11},{11... | collective-permute-start | bytes 196616 | tf_op jit(solution)/shard_map/ppermute | solution.py:18
  175.8 6.6 %collective-permute-start.14 = (f32[1,128,128]{2,1,0:T(8,128)S(1)}, f32[1,128,128]{2,1,0:T(8,128)S(1)}, u32[]{:S(2)}, u32[]{:S(2)}) collective-permute-start(f32[1,128,128]{2,1,0:T(8,128)S(1)} %get-tuple-element.130), channel_id=1, source_target_pairs={{1,0},{2,1},{3,2},{4,3},{5,4},{6,5},{7,6},{9,8},{10,9},{11,10},{12... | collective-permute-start | bytes 196616 | tf_op jit(solution)/shard_map/ppermute | solution.py:20
  177.1 6.2 %collective-permute-start.15 = (f32[1,128,128]{2,1,0:T(8,128)S(1)}, f32[1,128,128]{2,1,0:T(8,128)S(1)}, u32[]{:S(2)}, u32[]{:S(2)}) collective-permute-start(f32[1,128,128]{2,1,0:T(8,128)S(1)} %get-tuple-element.131), channel_id=1, source_target_pairs={{0,1},{1,2},{2,3},{3,4},{4,5},{5,6},{6,7},{8,9},{9,10},{10,11},{11... | collective-permute-start | bytes 196616 | tf_op jit(solution)/shard_map/ppermute | solution.py:18
  254.3 173.9 %reduce-scatter.9.cloned.1.call-start = ((), (), s32[]{:S(2)}) async-start(), calls=%async_computation.6 | async-start | bytes 2359296 | tf_op jit(solution)/shard_map/reduce_scatter | solution.py:104
  294.9 4.4 collective-permute-start.16
  300.6 4.4 collective-permute-start.18
  306.2 6.6 %collective-permute-start.20 = (f32[1,128,128]{2,1,0:T(8,128)S(1)}, f32[1,128,128]{2,1,0:T(8,128)S(1)}, u32[]{:S(2)}, u32[]{:S(2)}) collective-permute-start(f32[1,128,128]{2,1,0:T(8,128)S(1)} %get-tuple-element.92), channel_id=1, source_target_pairs={{1,0},{2,1},{3,2},{4,3},{5,4},{6,5},{7,6},{9,8},{10,9},{11,10},{12... | collective-permute-start | bytes 196616 | tf_op jit(solution)/shard_map/ppermute | solution.py:20
  307.5 6.2 %collective-permute-start.21 = (f32[1,128,128]{2,1,0:T(8,128)S(1)}, f32[1,128,128]{2,1,0:T(8,128)S(1)}, u32[]{:S(2)}, u32[]{:S(2)}) collective-permute-start(f32[1,128,128]{2,1,0:T(8,128)S(1)} %get-tuple-element.93), channel_id=1, source_target_pairs={{0,1},{1,2},{2,3},{3,4},{4,5},{5,6},{6,7},{8,9},{9,10},{10,11},{11... | collective-permute-start | bytes 196616 | tf_op jit(solution)/shard_map/ppermute | solution.py:18
  314.0 6.6 %collective-permute-start.22 = (f32[1,128,128]{2,1,0:T(8,128)S(1)}, f32[1,128,128]{2,1,0:T(8,128)S(1)}, u32[]{:S(2)}, u32[]{:S(2)}) collective-permute-start(f32[1,128,128]{2,1,0:T(8,128)S(1)} %get-tuple-element.82), channel_id=1, source_target_pairs={{1,0},{2,1},{3,2},{4,3},{5,4},{6,5},{7,6},{9,8},{10,9},{11,10},{12... | collective-permute-start | bytes 196616 | tf_op jit(solution)/shard_map/ppermute | solution.py:20
  315.3 6.2 %collective-permute-start.23 = (f32[1,128,128]{2,1,0:T(8,128)S(1)}, f32[1,128,128]{2,1,0:T(8,128)S(1)}, u32[]{:S(2)}, u32[]{:S(2)}) collective-permute-start(f32[1,128,128]{2,1,0:T(8,128)S(1)} %get-tuple-element.83), channel_id=1, source_target_pairs={{0,1},{1,2},{2,3},{3,4},{4,5},{5,6},{6,7},{8,9},{9,10},{10,11},{11... | collective-permute-start | bytes 196616 | tf_op jit(solution)/shard_map/ppermute | solution.py:18
  392.8 173.7 %reduce-scatter.11.cloned.1.call-start = ((), (), s32[]{:S(2)}) async-start(), calls=%async_computation.7 | async-start | bytes 2359296 | tf_op jit(solution)/shard_map/reduce_scatter | solution.py:104
  433.2 4.4 collective-permute-start.24
  438.8 4.4 collective-permute-start.26
  444.5 6.6 %collective-permute-start.28 = (f32[1,128,128]{2,1,0:T(8,128)S(1)}, f32[1,128,128]{2,1,0:T(8,128)S(1)}, u32[]{:S(2)}, u32[]{:S(2)}) collective-permute-start(f32[1,128,128]{2,1,0:T(8,128)S(1)} %get-tuple-element.44), channel_id=1, source_target_pairs={{1,0},{2,1},{3,2},{4,3},{5,4},{6,5},{7,6},{9,8},{10,9},{11,10},{12... | collective-permute-start | bytes 196616 | tf_op jit(solution)/shard_map/ppermute | solution.py:20
  445.8 6.2 %collective-permute-start.29 = (f32[1,128,128]{2,1,0:T(8,128)S(1)}, f32[1,128,128]{2,1,0:T(8,128)S(1)}, u32[]{:S(2)}, u32[]{:S(2)}) collective-permute-start(f32[1,128,128]{2,1,0:T(8,128)S(1)} %get-tuple-element.45), channel_id=1, source_target_pairs={{0,1},{1,2},{2,3},{3,4},{4,5},{5,6},{6,7},{8,9},{9,10},{10,11},{11... | collective-permute-start | bytes 196616 | tf_op jit(solution)/shard_map/ppermute | solution.py:18
  452.3 6.6 %collective-permute-start.30 = (f32[1,128,128]{2,1,0:T(8,128)S(1)}, f32[1,128,128]{2,1,0:T(8,128)S(1)}, u32[]{:S(2)}, u32[]{:S(2)}) collective-permute-start(f32[1,128,128]{2,1,0:T(8,128)S(1)} %get-tuple-element.34), channel_id=1, source_target_pairs={{1,0},{2,1},{3,2},{4,3},{5,4},{6,5},{7,6},{9,8},{10,9},{11,10},{12... | collective-permute-start | bytes 196616 | tf_op jit(solution)/shard_map/ppermute | solution.py:20
  453.6 6.2 %collective-permute-start.31 = (f32[1,128,128]{2,1,0:T(8,128)S(1)}, f32[1,128,128]{2,1,0:T(8,128)S(1)}, u32[]{:S(2)}, u32[]{:S(2)}) collective-permute-start(f32[1,128,128]{2,1,0:T(8,128)S(1)} %get-tuple-element.35), channel_id=1, source_target_pairs={{0,1},{1,2},{2,3},{3,4},{4,5},{5,6},{6,7},{8,9},{9,10},{10,11},{11... | collective-permute-start | bytes 196616 | tf_op jit(solution)/shard_map/ppermute | solution.py:18
  (14 other events, 189.1 us)
Sparse Core Ops, SparseCore 0:
  115.4 36.1 reduce-scatter.4
  254.4 35.4 reduce-scatter.6
  392.9 35.2 reduce-scatter.8
  531.2 35.2 reduce-scatter.10
